TPU v7x, 64 devices: a 2x2x8 block of a 4x4x8 slice. The times are simulated.
64 devices in a mesh: dp: 4 (over x, y), x: 16 (over z, core).
Axes of the slice: x: 2, y: 2, z: 8, core: 2. Of those that a mesh axis runs over, the one named last changes fastest.
The devices are a block of a 4x4x8 slice.
Arguments:
- c_raw: bfloat16 [512, 1024, 512], P('dp', 'x'), parts along dimension 0
- k_raw: bfloat16 [512, 1024, 64], P('dp', 'x'), parts along dimension 0
- norm_gain: bfloat16 [512], replicated
- rope_cos: float32 [1024, 32], P('x')
- rope_sin: float32 [1024, 32], P('x')
- seq_lens: int32 [512], P('dp'), parts along dimension 0
- q_lat: bfloat16 [512, 128, 512], P(('dp', 'x')), parts along dimension 0
- q_rope: bfloat16 [512, 128, 64], P(('dp', 'x')), parts along dimension 0
Outputs:
- output 1: bfloat16 [512, 1024, 512], P(('dp', 'x')), parts along dimension 0
- output 2: bfloat16 [512, 1024, 64], P(('dp', 'x')), parts along dimension 0
- output 3: bfloat16 [512, 128, 512], P(('dp', 'x')), parts along dimension 0
There are 4 independent parts. A program takes and returns all parts, laid end to end along the dimension named above; an argument that names none is the same for every part.
All inputs are finite; a program needn't handle non-finite values.
Results may differ from a plain program's by a relative error of at most 0.00587817.
Values are sent between devices in bfloat16 or wider.
A program may use at most 768 MiB of HBM per device.

v0:
```python
import jax
import jax.numpy as jnp
from jax import lax
from jax.sharding import PartitionSpec as P

NORM_EPS = 1e-6


def normed_rope(c_raw, k_raw, norm_gain, rope_cos, rope_sin, valid):
    lat_f32 = c_raw.astype(jnp.float32)
    inv_rms = lax.rsqrt(jnp.mean(lat_f32 * lat_f32, axis=-1, keepdims=True) + NORM_EPS)
    c_norm = jnp.where(valid[..., None], lat_f32 * inv_rms * norm_gain.astype(jnp.float32), 0.0)
    half_dim = k_raw.shape[-1] // 2
    key_f32 = k_raw.astype(jnp.float32)
    key_lo = key_f32[..., :half_dim]
    key_hi = key_f32[..., half_dim:]
    rotated = jnp.concatenate([key_lo * rope_cos - key_hi * rope_sin, key_hi * rope_cos + key_lo * rope_sin], axis=-1)
    k_rope = jnp.where(valid[..., None], rotated, 0.0)
    return c_norm.astype(jnp.bfloat16), k_rope.astype(jnp.bfloat16)


def latent_attention(q_lat, q_rope, c_cache, kr_cache, valid):
    attn_scale = (q_lat.shape[-1] + q_rope.shape[-1]) ** -0.5
    scores = jnp.einsum("rhk,rsk->rhs", q_lat, c_cache, preferred_element_type=jnp.float32)
    scores = scores + jnp.einsum("rhe,rse->rhs", q_rope, kr_cache, preferred_element_type=jnp.float32)
    scores = jnp.where(valid[:, None, :], scores * attn_scale, -1e30)
    weights = jnp.exp(scores - jnp.max(scores, axis=-1, keepdims=True))
    weight_sum = jnp.sum(weights, axis=-1)
    weighted = jnp.einsum("rhs,rsk->rhk", weights.astype(jnp.bfloat16), c_cache, preferred_element_type=jnp.float32)
    return (weighted / weight_sum[..., None]).astype(jnp.bfloat16)


def solution(mesh):
    seq_spec = P("dp", "x", None)
    req_spec = P(("dp", "x"), None, None)

    def local_step(c_raw, k_raw, norm_gain, rope_cos, rope_sin, seq_lens, q_lat, q_rope):
        dev_index = lax.axis_index("x")
        seq_local = c_raw.shape[1]
        req_local = q_lat.shape[0]
        positions = dev_index * seq_local + jnp.arange(seq_local)
        valid = positions[None, :] < seq_lens[:, None]
        c_norm, k_rope = normed_rope(c_raw, k_raw, norm_gain, rope_cos, rope_sin, valid)
        c_cache = lax.all_to_all(c_norm, "x", 0, 1, tiled=True)
        kr_cache = lax.all_to_all(k_rope, "x", 0, 1, tiled=True)
        own_lens = lax.dynamic_slice_in_dim(seq_lens, dev_index * req_local, req_local)
        own_valid = jnp.arange(c_cache.shape[1])[None, :] < own_lens[:, None]
        o_lat = latent_attention(q_lat, q_rope, c_cache, kr_cache, own_valid)
        return c_cache, kr_cache, o_lat

    return jax.shard_map(local_step, mesh=mesh, in_specs=(seq_spec, seq_spec, P(None), P("x", None), P("x", None), P("dp"), req_spec, req_spec), out_specs=(req_spec, req_spec, req_spec), check_vma=False)
```

profile of v0, /device:TPU:21, one launch (start us, length us, event | category | flops | bytes accessed | tf_op | source)
XLA Modules:
  0.0 271.3 jit_solution(11528548274047752966)
XLA Ops:
  0.6 0.0 copy-start
  0.7 0.0 copy-start.5
  0.7 0.0 copy-start.6
  0.7 0.0 copy-start.8
  0.7 4.0 %copy.18 = bf16[128,64,64]{2,1,0:T(8,128)(2,1)S(1)} copy(bf16[128,64,64]{0,2,1:T(8,128)(2,1)} %param.9) | data formatting | bytes 2097152 | tf_op args[1]
  4.7 2.5 convert_element_type.24
  7.2 0.0 copy-done.5
  7.2 0.1 copy.20
  7.3 0.0 copy-done.6
  7.3 0.1 copy.19
  7.4 0.0 copy-done.8
  7.4 0.1 broadcast_compare_fusion
  7.5 5.0 %multiply_subtract_fusion = (bf16[128,64,32]{2,1,0:T(8,128)(2,1)S(1)}, bf16[128,64,32]{2,1,0:T(8,128)(2,1)S(1)}) fusion(f32[128,64,64]{2,1,0:T(8,128)} %convert_element_type.24, f32[64,32]{1,0:T(8,128)S(1)} %copy.20, f32[64,32]{1,0:T(8,128)S(1)} %copy.19), kind=kLoop, calls=%fused_computation.13 | loop fusion | flops 2097152 | bytes 3162112 | tf_op jit(solution)/shard_map/sub | solution.py:17
  12.5 3.2 %fusion.4 = bf16[128,64,64]{2,1,0:T(8,128)(2,1)S(1)} fusion(bf16[128,64,32]{2,1,0:T(8,128)(2,1)S(1)} %get-tuple-element.4, bf16[128,64,32]{2,1,0:T(8,128)(2,1)S(1)} %get-tuple-element.3, pred[128,64]{1,0:T(8,128)(4,1)S(1)} %broadcast_compare_fusion), kind=kLoop, calls=%fused_computation.7 | loop fusion | flops 2621440 | bytes 2105344 | tf_op jit(solution)/shard_map/convert_element_type | solution.py:19
  15.6 0.0 copy-start.7
  15.7 2.2 reshape.68
  17.9 10.7 %all-to-all-start.1 = ((bf16[16,2,16384]{2,1,0:T(2,128)(2,1)}), bf16[16,2,16384]{2,1,0:T(2,128)(2,1)S(1)}, u32[]{:S(2)}, u32[]{:S(2)}) async-start(bf16[16,2,16384]{2,1,0:T(2,128)(2,1)} %reshape.68), calls=%async_computation.1 | async-start | bytes 2097152 | tf_op jit(solution)/shard_map/all_to_all | solution.py:45
  28.6 0.0 copy-done.7
  28.7 5.1 %fusion = f32[128,64]{1,0:T(8,128)S(1)} fusion(bf16[128,64,512]{2,1,0:T(8,128)(2,1)} %param.8), kind=kLoop, calls=%fused_computation.2 | loop fusion | flops 12574720 | bytes 8421376 | tf_op jit(solution)/shard_map/reduce_sum | solution.py:11
  33.8 10.0 %fusion.3 = bf16[128,64,512]{2,1,0:T(8,128)(2,1)} fusion(bf16[128,64,512]{2,1,0:T(8,128)(2,1)} %param.8, f32[512]{0:T(512)S(1)} %convert_element_type.22, f32[128,64]{1,0:T(8,128)S(1)} %add_rsqrt_fusion, pred[128,64]{1,0:T(8,128)(4,1)S(1)} %broadcast_compare_fusion), kind=kLoop, calls=%fused_computation.5 | loop fusion | flops 20971520 | bytes 16820224 | tf_op jit(solution)/shard_map/convert_element_type | solution.py:19
  43.8 12.7 %all-to-all-done.1 = bf16[16,2,16384]{2,1,0:T(2,128)(2,1)S(1)} async-done(((bf16[16,2,16384]{2,1,0:T(2,128)(2,1)}), bf16[16,2,16384]{2,1,0:T(2,128)(2,1)S(1)}, u32[]{:S(2)}, u32[]{:S(2)}) %all-to-all-start.1) | async-done | bytes 1048608 | tf_op jit(solution)/shard_map/all_to_all | solution.py:45
  56.5 0.0 copy-start.1
  56.5 1.0 copy-done.1
  57.5 5.0 %all-to-all-start = ((bf16[128,64,512]{2,1,0:T(8,128)(2,1)}), bf16[128,64,512]{2,1,0:T(8,128)(2,1)}, u32[]{:S(2)}, u32[]{:S(2)}) async-start(bf16[128,64,512]{2,1,0:T(8,128)(2,1)} %fusion.3), calls=%async_computation | async-start | bytes 16777216 | tf_op jit(solution)/shard_map/all_to_all | solution.py:44
  62.5 0.1 dynamic_slice.3
  62.6 0.1 iota_compare_fusion
  62.7 3.8 %reshape.69 = bf16[128,64,64]{2,1,0:T(8,128)(2,1)S(1)} reshape(bf16[16,2,16384]{2,1,0:T(2,128)(2,1)} %copy-done.1) | data formatting | bytes 2097152
  66.4 0.0 copy-start.4
  66.5 3.2 %copy.21 = bf16[8,16,64,64]{2,1,3,0:T(8,128)(2,1)} copy(bf16[8,16,64,64]{3,2,0,1:T(8,128)(2,1)S(1)} %bitcast.33) | data formatting | bytes 2097152 | tf_op jit(solution)/shard_map/all_to_all | solution.py:45
  69.7 3.2 %all_to_all.33 = bf16[8,1024,64]{1,2,0:T(8,128)(2,1)S(1)} reshape(bf16[8,16,64,64]{2,1,3,0:T(8,128)(2,1)} %copy.21) | data formatting | bytes 2097152 | tf_op jit(solution)/shard_map/all_to_all | solution.py:45
  72.9 0.0 copy-done.4
  72.9 0.0 copy-start.3
  73.0 2.8 %fusion.13 = f32[8,1024,128]{2,1,0:T(8,128)} fusion(bf16[8,1024,64]{1,2,0:T(8,128)(2,1)S(1)} %all_to_all.33, bf16[8,128,64]{1,2,0:T(8,128)(2,1)S(1)} %copy-done.4), kind=kOutput, calls=%fused_computation.23 | convolution fusion | flops 134217728 | bytes 5373952 | tf_op jit(solution)/shard_map/rhe,rse->rhs/dot_general | solution.py:25
  75.7 176.3 %all-to-all-done = bf16[128,64,512]{2,1,0:T(8,128)(2,1)} async-done(((bf16[128,64,512]{2,1,0:T(8,128)(2,1)}), bf16[128,64,512]{2,1,0:T(8,128)(2,1)}, u32[]{:S(2)}, u32[]{:S(2)}) %all-to-all-start) | async-done | bytes 8388640 | tf_op jit(solution)/shard_map/all_to_all | solution.py:44
  252.1 0.0 copy-start.2
  252.1 8.0 %copy.17 = bf16[16,8,64,512]{3,2,0,1:T(8,128)(2,1)} copy(bf16[16,8,64,512]{3,2,1,0:T(8,128)(2,1)} %bitcast) | data formatting | bytes 16777216 | tf_op jit(solution)/shard_map/all_to_all | solution.py:44
  260.1 0.0 copy-done.3
  260.1 0.0 slice-start
  260.1 0.0 copy-done
  260.1 0.0 copy-done.2
  260.1 0.0 slice-start.1
  260.1 7.7 %bitcast_reduce_fusion = (f32[8,128]{1,0:T(8,128)S(1)}, f32[8,1024,128]{2,1,0:T(8,128)S(1)}) fusion(f32[8,1024,128]{2,1,0:T(8,128)S(1)} %copy-done.2, bf16[8,1024,512]{2,1,0:T(8,128)(2,1)} %bitcast.28, bf16[8,128,512]{2,1,0:T(8,128)(2,1)S(1)} %copy-done, pred[8,1024]{1,0:T(8,128)(4,1)S(1)} %iota_compare_fusion), kind=kOutput, calls=%fused_computation.9 | convolution fusion | flops 1077935104 | bytes 17838080 | tf_op jit(solution)/shard_map/rhk,rsk->rhs/dot_general | solution.py:24
  267.9 0.6 fusion.6
  268.5 0.0 slice-done
  268.5 0.0 slice-done.1
  268.5 2.8 %divide_convert_fusion = bf16[8,128,512]{2,1,0:T(8,128)(2,1)} fusion(bf16[8,1024,512]{2,1,0:T(8,128)(2,1)S(1)} %bitcast.32, f32[8,1024,128]{2,1,0:T(8,128)S(1)} %get-tuple-element.6, f32[8,128]{1,0:T(8,128)S(1)} %get-tuple-element.5, f32[8,128]{1,0:T(8,128)S(1)} %fusion.6), kind=kOutput, calls=%fused_computation.17 | convolution fusion | flops 1076887552 | bytes 13639680 | tf_op jit(solution)/shard_map/rhs,rsk->rhk/dot_general | solution.py:29
  (4 shorter events, 0.0 us)
Async XLA Ops:
  0.6 259.5 %copy-start = (bf16[8,128,512]{2,1,0:T(8,128)(2,1)S(1)}, bf16[8,128,512]{2,1,0:T(8,128)(2,1)}, u32[]{:S(2)}) copy-start(bf16[8,128,512]{2,1,0:T(8,128)(2,1)} %param.14) | copy-start | bytes 3145732
  0.7 6.5 %copy-start.5 = (f32[64,32]{0,1:T(8,128)S(1)}, f32[64,32]{0,1:T(8,128)}, u32[]{:S(2)}) copy-start(f32[64,32]{0,1:T(8,128)} %param.12) | copy-start | bytes 24580
  0.7 6.6 %copy-start.6 = (f32[64,32]{0,1:T(8,128)S(1)}, f32[64,32]{0,1:T(8,128)}, u32[]{:S(2)}) copy-start(f32[64,32]{0,1:T(8,128)} %param.11) | copy-start | bytes 24580
  0.7 6.7 %copy-start.8 = (s32[128]{0:T(128)S(1)}, s32[128]{0:T(128)}, u32[]{:S(2)}) copy-start(s32[128]{0:T(128)} %param.13) | copy-start | bytes 1540
  15.6 13.0 %copy-start.7 = (bf16[512]{0:T(512)(128)(2,1)S(1)}, bf16[512]{0:T(512)(128)(2,1)}, u32[]{:S(2)}) copy-start(bf16[512]{0:T(512)(128)(2,1)} %param.10) | copy-start | bytes 3076
  17.9 38.6 %all-to-all-start.1 = ((bf16[16,2,16384]{2,1,0:T(2,128)(2,1)}), bf16[16,2,16384]{2,1,0:T(2,128)(2,1)S(1)}, u32[]{:S(2)}, u32[]{:S(2)}) async-start(bf16[16,2,16384]{2,1,0:T(2,128)(2,1)} %reshape.68), calls=%async_computation.1 | async-start | bytes 2097152 | tf_op jit(solution)/shard_map/all_to_all | solution.py:45
  56.5 1.0 copy-start.1
  57.5 194.6 %all-to-all-start = ((bf16[128,64,512]{2,1,0:T(8,128)(2,1)}), bf16[128,64,512]{2,1,0:T(8,128)(2,1)}, u32[]{:S(2)}, u32[]{:S(2)}) async-start(bf16[128,64,512]{2,1,0:T(8,128)(2,1)} %fusion.3), calls=%async_computation | async-start | bytes 16777216 | tf_op jit(solution)/shard_map/all_to_all | solution.py:44
  66.4 6.5 %copy-start.4 = (bf16[8,128,64]{1,2,0:T(8,128)(2,1)S(1)}, bf16[8,128,64]{1,2,0:T(8,128)(2,1)}, u32[]{:S(2)}) copy-start(bf16[8,128,64]{1,2,0:T(8,128)(2,1)} %param.15) | copy-start | bytes 393220
  72.9 187.2 %copy-start.3 = (bf16[8,1024,64]{1,2,0:T(8,128)(2,1)}, bf16[8,1024,64]{1,2,0:T(8,128)(2,1)S(1)}, u32[]{:S(2)}) copy-start(bf16[8,1024,64]{1,2,0:T(8,128)(2,1)S(1)} %all_to_all.33) | copy-start | bytes 3145732
  252.1 8.1 %copy-start.2 = (f32[8,1024,128]{2,1,0:T(8,128)S(1)}, f32[8,1024,128]{2,1,0:T(8,128)}, u32[]{:S(2)}) copy-start(f32[8,1024,128]{2,1,0:T(8,128)} %fusion.13) | copy-start | bytes 12582916
  260.1 8.3 %slice-start = ((s8[8388608]{0:T(1024)(128)(4,1)}), s8[4194304]{0:T(1024)(128)(4,1)S(1)}, s32[]{:S(2)}) async-start(s8[8388608]{0:T(1024)(128)(4,1)} %bitcast.30), calls=%async_computation.2 | async-start | bytes 8388608
  260.1 8.3 %slice-start.1 = ((s8[8388608]{0:T(1024)(128)(4,1)}), s8[4194304]{0:T(1024)(128)(4,1)S(1)}, s32[]{:S(2)}) async-start(s8[8388608]{0:T(1024)(128)(4,1)} %bitcast.30), calls=%async_computation.3 | async-start | bytes 8388608
where the time goes:
time: 272 us; the launch traced here: 271 us
  waiting for transfers between devices  189 us (69%)
  other arithmetic  26.5 us (10%)
  local copies, waits for them, and re-layouts  25.8 us (9%)
  starting transfers between devices  15.8 us (6%)
  matrix products  13.3 us (5%)
    all_to_all x1, waiting for transfers between devices, local_step(): c_cache = lax.all_to_all(c_norm, 'x', 0, 1, tiled=True)  176 us
    convert_element_type x2, other arithmetic, normed_rope(): return (c_norm.astype(jnp.bfloat16), k_rope.astype(jnp.bfloat16))  13.2 us
    all_to_all x1, waiting for transfers between devices, local_step(): kr_cache = lax.all_to_all(k_rope, 'x', 0, 1, tiled=True)  12.7 us
    unnamed x27, local copies, waits for them, and re-layouts  11.2 us
    all_to_all x1, starting transfers between devices, local_step(): kr_cache = lax.all_to_all(k_rope, 'x', 0, 1, tiled=True)  10.7 us
    all_to_all x1, local copies, waits for them, and re-layouts, local_step(): c_cache = lax.all_to_all(c_norm, 'x', 0, 1, tiled=True)  8.05 us
    dot_general x1, matrix products, latent_attention(): jnp.einsum('rhk,rsk->rhs', q_lat, c_cache, preferred_element_type=jnp.flo...  7.74 us
    all_to_all x2, local copies, waits for them, and re-layouts, local_step(): kr_cache = lax.all_to_all(k_rope, 'x', 0, 1, tiled=True)  6.47 us
  transfers between devices with their start and end apart: 2, of which 2 were waited for; matrix products, arithmetic and copies ran while one was open for 9% of the time, Pallas kernels for 0%

commit v1 on v0

v1 whole, which is shorter than its diff:
```python
import functools

import jax
import jax.numpy as jnp
from jax import lax
from jax.experimental import pallas as pl
from jax.experimental.pallas import tpu as pltpu
from jax.sharding import PartitionSpec as P

NORM_EPS = 1e-6
MESH = pl.DeviceIdType.MESH
LOOKAHEAD = 2


def partner_order(n):
    chips = n // 2
    order = [(0, 1)]
    for dist in range(1, chips // 2 + 1):
        for core in (0, 1):
            order.append((dist, core))
            if 2 * dist != chips:
                order.append((-dist, core))
    return order


def exchange_kernel(n, lens_ref, lens_row_ref, gain_ref, cos_ref, sin_ref, c_hbm, k_hbm, ql_hbm, qr_hbm, recv, kr_out, o_ref, send, k_raw, rot, turned, kr_send, kr_recv, q_lat, q_rope, load_sem, send_sem, recv_sem, kr_send_sem, kr_recv_sem):
    me = lax.axis_index("x")
    chips = n // 2
    my_chip, my_core = me // 2, lax.rem(me, 2)
    slots, _, seq_local, rank = send.shape
    half = cos_ref.shape[0]
    seq_len = recv.shape[1]
    attn_scale = (rank + 2 * half) ** -0.5
    partners = [2 * lax.rem(my_chip + dist + chips, chips) + lax.rem(my_core + core, 2) for dist, core in partner_order(n)]

    barrier = pltpu.get_barrier_semaphore()
    for target in partners:
        pl.semaphore_signal(barrier, inc=1, device_id={"x": target}, device_id_type=MESH)

    def load_c(slot):
        return pltpu.make_async_copy(c_hbm.at[:, slot], send.at[slot], load_sem.at[slot])

    load_k = pltpu.make_async_copy(k_hbm, k_raw, load_sem.at[slots])
    load_ql = pltpu.make_async_copy(ql_hbm, q_lat, load_sem.at[slots + 1])
    load_qr = pltpu.make_async_copy(qr_hbm, q_rope, load_sem.at[slots + 2])
    load_c(0).start()

    gain = gain_ref[...].astype(jnp.float32)
    row_pos = me * seq_local + lax.broadcasted_iota(jnp.int32, (seq_local, 1), 0)

    def norm_slot(slot):
        def one(dest, carry):
            rows = send[slot, dest].astype(jnp.float32)
            inv_rms = lax.rsqrt(jnp.mean(rows * rows, axis=-1, keepdims=True) + NORM_EPS)
            valid = row_pos < lens_ref[dest * slots + slot]
            normed = jnp.where(valid, rows * inv_rms * gain, 0.0).astype(jnp.bfloat16)
            send[slot, dest] = normed

            @pl.when(dest == me)
            def _():
                recv[slot, pl.ds(pl.multiple_of(me * seq_local, seq_local), seq_local)] = normed

            return carry

        lax.fori_loop(0, n, one, 0)

    def c_copy(slot, i):
        return pltpu.make_async_remote_copy(
            src_ref=send.at[slot, partners[i]],
            dst_ref=recv.at[slot, pl.ds(pl.multiple_of(me * seq_local, seq_local), seq_local)],
            send_sem=send_sem.at[slot, i],
            recv_sem=recv_sem.at[slot, i],
            device_id={"x": partners[i]},
            device_id_type=MESH,
        )

    def kr_copy(i):
        return pltpu.make_async_remote_copy(
            src_ref=kr_send.at[partners[i]],
            dst_ref=kr_recv.at[me],
            send_sem=kr_send_sem.at[i],
            recv_sem=kr_recv_sem.at[i],
            device_id={"x": partners[i]},
            device_id_type=MESH,
        )

    load_c(0).wait()
    load_k.start()
    for slot in range(1, slots):
        load_c(slot).start()
    load_ql.start()
    load_qr.start()
    norm_slot(0)
    pl.semaphore_wait(barrier, n - 1)
    for i in range(n - 1):
        c_copy(0, i).start()

    load_k.wait()
    lens_row = lens_row_ref[...]
    for pos in range(seq_local):
        lo = k_raw[pos, :half, :].astype(jnp.float32)
        hi = k_raw[pos, half:, :].astype(jnp.float32)
        cos = cos_ref[:, pos : pos + 1]
        sin = sin_ref[:, pos : pos + 1]
        valid = me * seq_local + pos < lens_row
        rot[2 * half * pos : 2 * half * pos + half, :] = jnp.where(valid, lo * cos - hi * sin, 0.0)
        rot[2 * half * pos + half : 2 * half * (pos + 1), :] = jnp.where(valid, hi * cos + lo * sin, 0.0)
    requests = n * slots
    for dim in range(half):
        lo = rot[pl.ds(dim, seq_local, stride=2 * half), :]
        hi = rot[pl.ds(half + dim, seq_local, stride=2 * half), :]
        turned[pl.ds(dim, requests, stride=half), :] = jnp.concatenate([lo, hi], axis=0).T
    for dest in range(n):
        kr_send[dest] = turned[dest * slots * half : (dest + 1) * slots * half, :].astype(jnp.bfloat16)
    kr_recv[me] = kr_send[me]

    for slot in range(1, LOOKAHEAD):
        load_c(slot).wait()
        norm_slot(slot)
    for i in range(n - 1):
        kr_copy(i).start()
    for slot in range(1, LOOKAHEAD):
        for i in range(n - 1):
            c_copy(slot, i).start()
    load_ql.wait()
    load_qr.wait()
    low_lanes = lax.broadcasted_iota(jnp.int32, (half, 2 * seq_local), 1) < seq_local
    key_pos = lax.broadcasted_iota(jnp.int32, (1, seq_len), 1)

    def one_slot(slot, carry):
        @pl.when(slot + LOOKAHEAD < slots)
        def _():
            ahead = slot + LOOKAHEAD
            load_c(ahead).wait()
            norm_slot(ahead)
            for i in range(n - 1):
                c_copy(ahead, i).start()

        @pl.when(slot == 0)
        def _():
            for i in range(n - 1):
                kr_copy(i).wait_recv()

        for pair in range(chips):
            even = kr_recv[2 * pair, pl.ds(pl.multiple_of(slot * half, half), half), :].astype(jnp.float32)
            odd = kr_recv[2 * pair + 1, pl.ds(pl.multiple_of(slot * half, half), half), :].astype(jnp.float32)
            lanes = slice(2 * seq_local * pair, 2 * seq_local * (pair + 1))
            kr_out[slot, :half, lanes] = jnp.where(low_lanes, even, pltpu.roll(odd, seq_local, 1)).astype(jnp.bfloat16)
            kr_out[slot, half:, lanes] = jnp.where(low_lanes, pltpu.roll(even, seq_local, 1), odd).astype(jnp.bfloat16)
        rope_q = q_rope[slot].astype(jnp.float32).T.astype(jnp.bfloat16)
        scores = jnp.dot(rope_q, kr_out[slot], preferred_element_type=jnp.float32)

        for i in range(n - 1):
            c_copy(slot, i).wait_recv()
        cache = recv[slot]
        scores += lax.dot_general(q_lat[slot], cache, (((1,), (1,)), ((), ())), preferred_element_type=jnp.float32)
        valid = key_pos < lens_ref[me * slots + slot]
        scores = jnp.where(valid, scores * attn_scale, -1e30)
        weights = jnp.exp(scores - jnp.max(scores, axis=-1, keepdims=True))
        weight_sum = jnp.sum(weights, axis=-1, keepdims=True)
        weighted = jnp.dot(weights.astype(jnp.bfloat16), cache, preferred_element_type=jnp.float32)
        o_ref[slot] = (weighted / weight_sum).astype(jnp.bfloat16)
        return carry

    lax.fori_loop(0, slots, one_slot, 0)
    for i in range(n - 1):
        kr_copy(i).wait_send()

    def drain(slot, carry):
        for i in range(n - 1):
            c_copy(slot, i).wait_send()
        return carry

    lax.fori_loop(0, slots, drain, 0)


def store_kernel(c_ref, kr_ref, o_ref, c_out, kr_out, o_out, sem):
    copies = [pltpu.make_async_copy(src, dst, sem.at[i]) for i, (src, dst) in enumerate([(c_ref, c_out), (kr_ref, kr_out), (o_ref, o_out)])]
    for copy in copies:
        copy.start()
    for copy in copies:
        copy.wait()


def solution(mesh):
    n = mesh.shape["x"]
    seq_spec = P("dp", "x", None)
    req_spec = P(("dp", "x"), None, None)

    def local_step(c_raw, k_raw, norm_gain, rope_cos, rope_sin, seq_lens, q_lat, q_rope):
        requests, seq_local, rank = c_raw.shape
        slots, heads, _ = q_lat.shape
        rope_dim = k_raw.shape[-1]
        half = rope_dim // 2
        seq_len = n * seq_local
        bf16, f32 = jnp.bfloat16, jnp.float32
        hbm = pl.BlockSpec(memory_space=pltpu.HBM)
        vmem = pl.BlockSpec(memory_space=pltpu.VMEM)
        smem = pl.BlockSpec(memory_space=pltpu.SMEM)
        outs = [((slots, seq_len, rank), bf16), ((slots, rope_dim, seq_len), bf16), ((slots, heads, rank), bf16)]
        c_got, kr_got, o_got = pl.pallas_call(
            functools.partial(exchange_kernel, n),
            out_shape=[pltpu.VMEM(*out) for out in outs],
            in_specs=[smem, vmem, vmem, vmem, vmem, hbm, hbm, hbm, hbm],
            out_specs=[vmem] * 3,
            scratch_shapes=[
                pltpu.VMEM((slots, n, seq_local, rank), bf16),
                pltpu.VMEM((seq_local, rope_dim, requests), bf16),
                pltpu.VMEM((seq_local * rope_dim, requests), f32),
                pltpu.VMEM((requests * half, 2 * seq_local), f32),
                pltpu.VMEM((n, slots * half, 2 * seq_local), bf16),
                pltpu.VMEM((n, slots * half, 2 * seq_local), bf16),
                pltpu.VMEM(q_lat.shape, bf16),
                pltpu.VMEM((slots, rope_dim, heads), bf16),
                pltpu.SemaphoreType.DMA((slots + 3,)),
                pltpu.SemaphoreType.DMA((slots, n - 1)),
                pltpu.SemaphoreType.DMA((slots, n - 1)),
                pltpu.SemaphoreType.DMA((n - 1,)),
                pltpu.SemaphoreType.DMA((n - 1,)),
            ],
            compiler_params=pltpu.CompilerParams(collective_id=0, has_side_effects=True, vmem_limit_bytes=40 * 1024 * 1024),
            name="exchange",
        )(
            seq_lens,
            seq_lens.reshape(1, requests),
            norm_gain.reshape(1, rank),
            rope_cos.T,
            rope_sin.T,
            c_raw.reshape(n, slots, seq_local, rank),
            jnp.transpose(k_raw, (1, 2, 0)),
            q_lat,
            jnp.transpose(q_rope, (0, 2, 1)),
        )
        c_cache, kr_cache, o_lat = pl.pallas_call(
            store_kernel,
            out_shape=[jax.ShapeDtypeStruct(*out) for out in outs],
            in_specs=[vmem] * 3,
            out_specs=[hbm] * 3,
            scratch_shapes=[pltpu.SemaphoreType.DMA((3,))],
            compiler_params=pltpu.CompilerParams(vmem_limit_bytes=8 * 1024 * 1024),
            name="store",
        )(c_got, kr_got, o_got)
        return c_cache, jnp.transpose(kr_cache, (0, 2, 1)), o_lat

    return jax.shard_map(local_step, mesh=mesh, in_specs=(seq_spec, seq_spec, P(None), P("x", None), P("x", None), P("dp"), req_spec, req_spec), out_specs=(req_spec, req_spec, req_spec), check_vma=False)
```

time: 272 us -> 233 us (0.86)
  Pallas kernels: 0 us -> 226 us
  waiting for transfers between devices: 189 us -> 0 us
  other arithmetic: 26.5 us -> 0 us
  local copies, waits for them, and re-layouts: 25.8 us -> 6.12 us
  starting transfers between devices: 15.8 us -> 0 us
  matrix products: 13.3 us -> 0 us
    pallas_call x0 -> x2, Pallas kernels: none -> 226 us  [the longest x1 222 us: local_step(): pl.pallas_call(functools.partial(exchange_kernel, n), out_shape=[pltpu.VM...]
    all_to_all x2 -> x0, waiting for transfers between devices: 189 us -> none  [the longest x1 176 us: local_step(): c_cache = lax.all_to_all(c_norm, 'x', 0, 1, tiled=True)]
    all_to_all x2 -> x0, starting transfers between devices: 15.8 us -> none  [the longest x1 10.7 us: local_step(): kr_cache = lax.all_to_all(k_rope, 'x', 0, 1, tiled=True)]
    convert_element_type x4 -> x0, other arithmetic: 15.6 us -> none  [the longest x2 13.2 us: normed_rope(): return (c_norm.astype(jnp.bfloat16), k_rope.astype(jnp.bfloat16))]
    all_to_all x3 -> x0, local copies, waits for them, and re-layouts: 14.5 us -> none  [the longest x1 8.05 us: local_step(): c_cache = lax.all_to_all(c_norm, 'x', 0, 1, tiled=True)]
    dot_general x3 -> x0, matrix products: 13.3 us -> none  [the longest x1 7.74 us: latent_attention(): jnp.einsum('rhk,rsk->rhs', q_lat, c_cache, preferred_element_type=jnp.flo...]
    unnamed x27 -> x12, local copies, waits for them, and re-layouts: 11.2 us -> 5.44 us
    reduce_sum x2 -> x0, other arithmetic: 5.67 us -> none  [the longest x1 5.1 us: normed_rope(): jnp.mean(lat_f32 * lat_f32, axis=-1, keepdims=True) + NORM_EPS]
  transfers between devices with their start and end apart: 2 -> 0, of which waited for: 2 -> 0; matrix products, arithmetic and copies ran while one was open for 9% -> 0% of each run, Pallas kernels for 0% -> 0%
where the time goes in v1:
time: 233 us
  Pallas kernels  226 us (97%)
  local copies, waits for them, and re-layouts  6.12 us (3%)
    pallas_call x1, Pallas kernels, local_step(): pl.pallas_call(functools.partial(exchange_kernel, n), out_shape=[pltpu.VM...  222 us
    unnamed x12, local copies, waits for them, and re-layouts  5.44 us

profile of v1, /device:TPU:21, one launch (start us, length us, event | category | flops | bytes accessed | tf_op | source)
XLA Modules:
  0.0 232.7 jit_solution(15575953204383886287)
XLA Ops:
  0.6 0.7 reshape.16.gain_ref
  1.3 0.0 copy-start
  1.3 1.2 copy-done
  2.5 0.0 copy-start.1
  2.5 1.2 copy-done.1
  3.8 0.0 copy-start.2
  3.8 0.9 copy-done.2
  4.7 0.0 copy-start.3
  4.7 0.7 copy-done.3
  5.4 0.0 copy-start.4
  5.4 0.7 copy-done.4
  6.1 0.0 copy-start.5
  6.1 0.7 copy-done.5
  6.8 221.9 %exchange.1 = (bf16[8,1024,512]{2,1,0:T(8,128)(2,1)S(1)}, bf16[8,64,1024]{2,1,0:T(8,128)(2,1)S(1)}, bf16[8,128,512]{2,1,0:T(8,128)(2,1)S(1)}) custom-call(s32[128]{0:T(128)S(1)} %copy-done.5, s32[1,128]{1,0:T(1,128)S(1)} %bitcast.11, bf16[1,512]{1,0:T(2,128)(2,1)S(1)} %reshape.16.gain_ref, f32[32,64]{1,0:T(8,128)S(1)} %bitcast.9, f32[32,64]{1,0:T(8,128)S(1)} %bitcast.10, ...), custom_call_target="tpu_custom_call" | custom-call | tf_op jit(solution)/shard_map/exchange/pallas_call | solution.py:201
  228.7 4.1 %store.1 = (bf16[8,1024,512]{2,1,0:T(8,128)(2,1)}, bf16[8,64,1024]{2,1,0:T(8,128)(2,1)}, bf16[8,128,512]{2,1,0:T(8,128)(2,1)}) custom-call(bf16[8,1024,512]{2,1,0:T(8,128)(2,1)S(1)} %get-tuple-element.9.c_ref, bf16[8,64,1024]{2,1,0:T(8,128)(2,1)S(1)} %get-tuple-element.10.kr_ref, bf16[8,128,512]{2,1,0:T(8,128)(2,1)S(1)} %get-tuple-element.11.o_ref), custom_call_target="tpu_custom_call" | custom-call | tf_op jit(solution)/shard_map/store/pallas_call | solution.py:234
Async XLA Ops:
  1.3 1.2 copy-start
  2.5 1.2 copy-start.1
  3.8 0.9 copy-start.2
  4.7 0.7 copy-start.3
  5.4 0.7 copy-start.4
  6.1 0.7 copy-start.5

commit v2 on v0

v2 whole, which is shorter than its diff:
```python
import functools

import jax
import jax.numpy as jnp
from jax import lax
from jax.experimental import pallas as pl
from jax.experimental.pallas import tpu as pltpu
from jax.sharding import PartitionSpec as P

NORM_EPS = 1e-6
MASKED = -3.0e38
MESH = pl.DeviceIdType.MESH


def message_order(chips, slots):
    order = []
    for dist in range(1, chips // 2):
        for core in (0, 1):
            for sign in (1, -1):
                order.append((sign * dist, core, 0, slots))
    order.insert(4, (0, 1, 0, slots))
    for first in (0, slots // 2):
        for core in (0, 1):
            order.append((chips // 2, core, first, slots // 2))
    return order


def attend_chunk(r, chip, q_lat, rope_q, recv, kr_out, acc, top, total, own_lens, attn_scale):
    width = own_lens.shape[-1]
    start = pl.multiple_of(chip * width, width)
    rows = recv[r, pl.ds(start, width), :]
    keys = kr_out[r, :, pl.ds(start, width)]
    scores = lax.dot_general(q_lat[r], rows, (((1,), (1,)), ((), ())), preferred_element_type=jnp.float32)
    scores += jnp.dot(rope_q[r], keys, preferred_element_type=jnp.float32)
    pos = start + lax.broadcasted_iota(jnp.int32, (1, width), 1)
    valid = pos < own_lens[r]
    scores = jnp.where(valid, scores * attn_scale, MASKED)
    old_top = top[r]
    new_top = jnp.maximum(old_top, jnp.max(scores, axis=-1, keepdims=True))
    weights = jnp.where(valid, jnp.exp(scores - new_top), 0.0)
    decay = jnp.exp(old_top - new_top)
    top[r] = new_top
    new_total = total[r] * decay + jnp.sum(weights, axis=-1, keepdims=True)
    total[r] = new_total
    mixed = acc[r] * decay + jnp.dot(weights.astype(jnp.bfloat16), rows, preferred_element_type=jnp.float32)
    return mixed, new_total


def exchange_kernel(n, lens_hbm, lens_row_hbm, gain_hbm, cos_hbm, sin_hbm, c_hbm, k_hbm, ql_hbm, qr_hbm, recv, kr_out, acc, top, total, q_lat, rope_q, own_lens, lens, lens_row, gain_ref, cos_ref, sin_ref, send, k_raw, rot, turned, kr_send, kr_recv, q_rope, small_sem, load_sem, send_sem, recv_sem, kr_send_sem, kr_recv_sem):
    me = lax.axis_index("x")
    chips = n // 2
    my_chip, my_core = me // 2, lax.rem(me, 2)
    _, slots, seq_local, rank = send.shape
    half = cos_ref.shape[0]
    attn_scale = (rank + 2 * half) ** -0.5
    messages = message_order(chips, slots)

    def device(dist, core):
        return 2 * lax.rem(my_chip + dist + chips, chips) + lax.rem(my_core + core, 2)

    partners = []
    for dist, core, _, _ in messages:
        if (dist, core) not in partners:
            partners.append((dist, core))
    targets = [device(*partner) for partner in partners]

    barrier = pltpu.get_barrier_semaphore()
    for target in targets:
        pl.semaphore_signal(barrier, inc=1, device_id={"x": target}, device_id_type=MESH)

    def load_c(i):
        dest = me if i == n - 1 else targets[i]
        return pltpu.make_async_copy(c_hbm.at[dest], send.at[dest], load_sem.at[i])

    small = [(lens_hbm, lens), (gain_hbm, gain_ref), (lens_row_hbm, lens_row), (cos_hbm, cos_ref), (sin_hbm, sin_ref), (k_hbm, k_raw), (qr_hbm, q_rope), (ql_hbm, q_lat)]
    small = [pltpu.make_async_copy(src, dst, small_sem.at[i]) for i, (src, dst) in enumerate(small)]
    for copy in small[:2]:
        copy.start()
    for i in range(4):
        load_c(i).start()
    for copy in small[2:]:
        copy.start()
    for i in range(4, n):
        load_c(i).start()
    for copy in small[:2]:
        copy.wait()

    gain = gain_ref[...].astype(jnp.float32).reshape(1, rank)
    row_pos = me * seq_local + lax.broadcasted_iota(jnp.int32, (seq_local, 1), 0)

    def norm_rows(i):
        load_c(i).wait()
        dest = me if i == n - 1 else targets[i]

        def one(slot, carry):
            rows = send[dest, slot].astype(jnp.float32)
            inv_rms = lax.rsqrt(jnp.mean(rows * rows, axis=-1, keepdims=True) + NORM_EPS)
            valid = row_pos < lens[dest * slots + slot]
            normed = jnp.where(valid, rows * inv_rms * gain, 0.0).astype(jnp.bfloat16)
            if i == n - 1:
                recv[slot, pl.ds(pl.multiple_of(me * seq_local, seq_local), seq_local), :] = normed
            else:
                send[dest, slot] = normed
            return carry

        lax.fori_loop(0, slots, one, 0, unroll=2)

    def c_copy(m):
        dist, core, first, count = messages[m]
        target = device(dist, core)
        return pltpu.make_async_remote_copy(
            src_ref=send.at[target, pl.ds(first, count)],
            dst_ref=recv.at[pl.ds(first, count), pl.ds(pl.multiple_of(me * seq_local, seq_local), seq_local)],
            send_sem=send_sem.at[m],
            recv_sem=recv_sem.at[m],
            device_id={"x": target},
            device_id_type=MESH,
        )

    def kr_copy(i):
        return pltpu.make_async_remote_copy(
            src_ref=kr_send.at[targets[i]],
            dst_ref=kr_recv.at[me],
            send_sem=kr_send_sem.at[i],
            recv_sem=kr_recv_sem.at[i],
            device_id={"x": targets[i]},
            device_id_type=MESH,
        )

    def send_rows(i):
        for m, (dist, core, _, _) in enumerate(messages):
            if (dist, core) == partners[i]:
                c_copy(m).start()

    early = 5
    norm_rows(0)
    norm_rows(1)
    pl.semaphore_wait(barrier, n - 1)
    for i in range(2, early):
        send_rows(i - 2)
        norm_rows(i)
    send_rows(early - 2)
    send_rows(early - 1)

    for copy in small[2:]:
        copy.wait()
    lens_vec = lens_row[...]
    for pos in range(seq_local):
        lo = k_raw[pos, :half, :].astype(jnp.float32)
        hi = k_raw[pos, half:, :].astype(jnp.float32)
        cos = cos_ref[:, pos : pos + 1]
        sin = sin_ref[:, pos : pos + 1]
        valid = me * seq_local + pos < lens_vec
        rot[2 * half * pos : 2 * half * pos + half, :] = jnp.where(valid, lo * cos - hi * sin, 0.0)
        rot[2 * half * pos + half : 2 * half * (pos + 1), :] = jnp.where(valid, hi * cos + lo * sin, 0.0)
    requests = n * slots
    for dim in range(half):
        lo = rot[pl.ds(dim, seq_local, stride=2 * half), :]
        hi = rot[pl.ds(half + dim, seq_local, stride=2 * half), :]
        turned[pl.ds(dim, requests, stride=half), :] = jnp.concatenate([lo, hi], axis=0).T
    for dest in range(n):
        kr_send[dest] = turned[dest * slots * half : (dest + 1) * slots * half, :].astype(jnp.bfloat16)
    kr_recv[me] = kr_send[me]

    norm_rows(early)
    for i in range(n - 1):
        kr_copy(i).start()
    for i in range(early + 1, n - 1):
        send_rows(i - 1)
        norm_rows(i)
    send_rows(n - 2)
    norm_rows(n - 1)

    for slot in range(slots):
        rope_q[slot] = q_rope[slot].astype(jnp.float32).T.astype(jnp.bfloat16)
        own_lens[slot] = jnp.full(own_lens.shape[1:], lens[me * slots + slot], jnp.int32)
    acc[...] = jnp.zeros_like(acc)
    top[...] = jnp.full_like(top, MASKED)
    total[...] = jnp.zeros_like(total)

    low_lanes = lax.broadcasted_iota(jnp.int32, (half, 2 * seq_local), 1) < seq_local

    def gather_chip(dist):
        chip = lax.rem(my_chip + dist + chips, chips)
        for i, (far, _) in enumerate(partners):
            if (far + dist) % chips == 0:
                kr_copy(i).wait_recv()
        start = pl.multiple_of(chip * 2 * seq_local, 2 * seq_local)
        for slot in range(slots):
            even = kr_recv[2 * chip, slot * half : (slot + 1) * half, :].astype(jnp.float32)
            odd = kr_recv[2 * chip + 1, slot * half : (slot + 1) * half, :].astype(jnp.float32)
            kr_out[slot, :half, pl.ds(start, 2 * seq_local)] = jnp.where(low_lanes, even, pltpu.roll(odd, seq_local, 1)).astype(jnp.bfloat16)
            kr_out[slot, half:, pl.ds(start, 2 * seq_local)] = jnp.where(low_lanes, pltpu.roll(even, seq_local, 1), odd).astype(jnp.bfloat16)
        for m, (far, _, _, _) in enumerate(messages):
            if (far + dist) % chips == 0:
                c_copy(m).wait_recv()
        return chip

    for dist in [0] + [sign * far for far in range(1, chips // 2) for sign in (1, -1)]:
        chip = gather_chip(dist)

        def one_request(r, carry, chip=chip):
            acc[r], _ = attend_chunk(r, chip, q_lat, rope_q, recv, kr_out, acc, top, total, own_lens, attn_scale)
            return carry

        lax.fori_loop(0, slots, one_request, 0, unroll=2)

    for i in range(n - 1):
        kr_copy(i).wait_send()
    gather_chip(chips // 2)
    for m in range(len(messages)):
        c_copy(m).wait_send()


def finish_kernel(n, attn_scale, recv, kr_in, acc, top_in, total_in, q_lat, rope_q, own_lens, c_out, kr_out, o_out, top, total, o_ref, sem):
    chips = n // 2
    slots = acc.shape[0]
    copies = [pltpu.make_async_copy(recv.at[r], c_out.at[r], sem.at[r]) for r in range(slots)]
    copies.append(pltpu.make_async_copy(kr_in, kr_out, sem.at[slots]))
    for copy in copies:
        copy.start()
    top[...] = top_in[...]
    total[...] = total_in[...]
    chip = lax.rem(lax.axis_index("x") // 2 + chips // 2, chips)
    for r in range(slots):
        mixed, weight_sum = attend_chunk(r, chip, q_lat, rope_q, recv, kr_in, acc, top, total, own_lens, attn_scale)
        o_ref[r] = (mixed / weight_sum).astype(jnp.bfloat16)
        copies.append(pltpu.make_async_copy(o_ref.at[r], o_out.at[r], sem.at[slots + 1 + r]))
        copies[-1].start()
    for copy in copies:
        copy.wait()


def solution(mesh):
    n = mesh.shape["x"]
    seq_spec = P("dp", "x", None)
    req_spec = P(("dp", "x"), None, None)

    def local_step(c_raw, k_raw, norm_gain, rope_cos, rope_sin, seq_lens, q_lat, q_rope):
        requests, seq_local, rank = c_raw.shape
        slots, heads, _ = q_lat.shape
        rope_dim = k_raw.shape[-1]
        half = rope_dim // 2
        seq_len = n * seq_local
        bf16, f32, i32 = jnp.bfloat16, jnp.float32, jnp.int32
        hbm = pl.BlockSpec(memory_space=pltpu.HBM)
        vmem = pl.BlockSpec(memory_space=pltpu.VMEM)
        messages = len(message_order(n // 2, slots))
        passed = [
            ((slots, seq_len, rank), bf16),
            ((slots, rope_dim, seq_len), bf16),
            ((slots, heads, rank), f32),
            ((slots, heads, 1), f32),
            ((slots, heads, 1), f32),
            ((slots, heads, rank), bf16),
            ((slots, heads, rope_dim), bf16),
            ((slots, 1, 2 * seq_local), i32),
        ]
        operands = (
            seq_lens,
            seq_lens.reshape(1, requests),
            norm_gain,
            rope_cos.T,
            rope_sin.T,
            c_raw.reshape(n, slots, seq_local, rank),
            jnp.transpose(k_raw, (1, 2, 0)),
            q_lat,
            jnp.transpose(q_rope, (0, 2, 1)),
        )
        got = pl.pallas_call(
            functools.partial(exchange_kernel, n),
            out_shape=[pltpu.VMEM(*out) for out in passed],
            in_specs=[hbm] * len(operands),
            out_specs=[vmem] * len(passed),
            scratch_shapes=[
                pltpu.SMEM((requests,), i32),
                pltpu.VMEM((1, requests), i32),
                pltpu.VMEM((rank,), bf16),
                pltpu.VMEM((half, seq_local), f32),
                pltpu.VMEM((half, seq_local), f32),
                pltpu.VMEM((n, slots, seq_local, rank), bf16),
                pltpu.VMEM((seq_local, rope_dim, requests), bf16),
                pltpu.VMEM((seq_local * rope_dim, requests), f32),
                pltpu.VMEM((requests * half, 2 * seq_local), f32),
                pltpu.VMEM((n, slots * half, 2 * seq_local), bf16),
                pltpu.VMEM((n, slots * half, 2 * seq_local), bf16),
                pltpu.VMEM((slots, rope_dim, heads), bf16),
                pltpu.SemaphoreType.DMA((8,)),
                pltpu.SemaphoreType.DMA((n,)),
                pltpu.SemaphoreType.DMA((messages,)),
                pltpu.SemaphoreType.DMA((messages,)),
                pltpu.SemaphoreType.DMA((n - 1,)),
                pltpu.SemaphoreType.DMA((n - 1,)),
            ],
            compiler_params=pltpu.CompilerParams(collective_id=0, has_side_effects=True, vmem_limit_bytes=40 * 1024 * 1024),
            name="exchange",
        )(*[pltpu.with_memory_space_constraint(x, pltpu.HBM) for x in operands])
        outs = [((slots, seq_len, rank), bf16), ((slots, rope_dim, seq_len), bf16), ((slots, heads, rank), bf16)]
        c_cache, kr_cache, o_lat = pl.pallas_call(
            functools.partial(finish_kernel, n, (rank + rope_dim) ** -0.5),
            out_shape=[jax.ShapeDtypeStruct(*out) for out in outs],
            in_specs=[vmem] * len(passed),
            out_specs=[hbm] * 3,
            scratch_shapes=[
                pltpu.VMEM((slots, heads, 1), f32),
                pltpu.VMEM((slots, heads, 1), f32),
                pltpu.VMEM((slots, heads, rank), bf16),
                pltpu.SemaphoreType.DMA((2 * slots + 1,)),
            ],
            compiler_params=pltpu.CompilerParams(vmem_limit_bytes=8 * 1024 * 1024),
            name="finish",
        )(*got)
        return c_cache, jnp.transpose(kr_cache, (0, 2, 1)), o_lat

    return jax.shard_map(local_step, mesh=mesh, in_specs=(seq_spec, seq_spec, P(None), P("x", None), P("x", None), P("dp"), req_spec, req_spec), out_specs=(req_spec, req_spec, req_spec), check_vma=False)
```

time: 272 us -> 222 us (0.82)
  Pallas kernels: 0 us -> 221 us
  waiting for transfers between devices: 189 us -> 0 us
  other arithmetic: 26.5 us -> 0 us
  local copies, waits for them, and re-layouts: 25.8 us -> 0 us
  starting transfers between devices: 15.8 us -> 0 us
  matrix products: 13.3 us -> 0 us
    pallas_call x0 -> x2, Pallas kernels: none -> 221 us  [the longest x1 217 us: local_step(): pl.pallas_call(functools.partial(exchange_kernel, n), out_shape=[pltpu.VM...]
    all_to_all x2 -> x0, waiting for transfers between devices: 189 us -> none  [the longest x1 176 us: local_step(): c_cache = lax.all_to_all(c_norm, 'x', 0, 1, tiled=True)]
    all_to_all x2 -> x0, starting transfers between devices: 15.8 us -> none  [the longest x1 10.7 us: local_step(): kr_cache = lax.all_to_all(k_rope, 'x', 0, 1, tiled=True)]
    convert_element_type x4 -> x0, other arithmetic: 15.6 us -> none  [the longest x2 13.2 us: normed_rope(): return (c_norm.astype(jnp.bfloat16), k_rope.astype(jnp.bfloat16))]
    all_to_all x3 -> x0, local copies, waits for them, and re-layouts: 14.5 us -> none  [the longest x1 8.05 us: local_step(): c_cache = lax.all_to_all(c_norm, 'x', 0, 1, tiled=True)]
    dot_general x3 -> x0, matrix products: 13.3 us -> none  [the longest x1 7.74 us: latent_attention(): jnp.einsum('rhk,rsk->rhs', q_lat, c_cache, preferred_element_type=jnp.flo...]
    unnamed x27 -> x0, local copies, waits for them, and re-layouts: 11.2 us -> none
    reduce_sum x2 -> x0, other arithmetic: 5.67 us -> none  [the longest x1 5.1 us: normed_rope(): jnp.mean(lat_f32 * lat_f32, axis=-1, keepdims=True) + NORM_EPS]
  transfers between devices with their start and end apart: 2 -> 0, of which waited for: 2 -> 0; matrix products, arithmetic and copies ran while one was open for 9% -> 0% of each run, Pallas kernels for 0% -> 0%
where the time goes in v2:
time: 222 us
  Pallas kernels  221 us (100%)
    pallas_call x1, Pallas kernels, local_step(): pl.pallas_call(functools.partial(exchange_kernel, n), out_shape=[pltpu.VM...  217 us

profile of v2, /device:TPU:21, one launch (start us, length us, event | category | flops | bytes accessed | tf_op | source)
XLA Modules:
  0.0 221.7 jit_solution(4340517007937261162)
XLA Ops:
  0.6 217.0 %exchange.1 = (bf16[8,1024,512]{2,1,0:T(8,128)(2,1)S(1)}, bf16[8,64,1024]{2,1,0:T(8,128)(2,1)S(1)}, f32[8,128,512]{2,1,0:T(8,128)S(1)}, f32[8,128,1]{2,1,0:T(8,1...) custom-call(s32[128]{0:T(128)} %lens_hbm.1, ...), custom_call_target="tpu_custom_call" | custom-call | tf_op jit(solution)/shard_map/exchange/pallas_call | solution.py:270
  217.7 4.0 %finish.1 = (bf16[8,1024,512]{2,1,0:T(8,128)(2,1)}, bf16[8,64,1024]{2,1,0:T(8,128)(2,1)}, bf16[8,128,512]{2,1,0:T(8,128)(2,1)}) custom-call(bf16[8,1024,512]{2,1,0:T(8,128)(2,1)S(1)} %get-tuple-element.14.recv, bf16[8,64,1024]{2,1,0:T(8,128)(2,1)S(1)} %get-tuple-element.15.kr_in, f32[8,128,512]{2,1,0:T(8,128)S(1)} %get-tuple-element.16.acc, ...), custom_call_target="tpu_custom_call" | custom-call | tf_op jit(solution)/shard_map/finish/pallas_call | solution.py:299

commit v3 on v2

--- a/solution.py
+++ b/solution.py
@@ -10,19 +10,29 @@
 NORM_EPS = 1e-6
 MASKED = -3.0e38
 MESH = pl.DeviceIdType.MESH
+DISTANCES = (1, 3, 2)
+RAW = 2
 
 
 def message_order(chips, slots):
+    far = chips // 2
     order = []
-    for dist in range(1, chips // 2):
+    for dist in DISTANCES:
         for core in (0, 1):
             for sign in (1, -1):
                 order.append((sign * dist, core, 0, slots))
     order.insert(4, (0, 1, 0, slots))
     for first in (0, slots // 2):
         for core in (0, 1):
-            order.append((chips // 2, core, first, slots // 2))
+            order.append((far, core, first, slots // 2))
     return order
+
+
+def normed_rows(rows, gain, first_pos, length):
+    rows = rows.astype(jnp.float32)
+    inv_rms = lax.rsqrt(jnp.mean(rows * rows, axis=-1, keepdims=True) + NORM_EPS)
+    valid = first_pos + lax.broadcasted_iota(jnp.int32, (rows.shape[0], 1), 0) < length
+    return jnp.where(valid, rows * inv_rms * gain, 0.0).astype(jnp.bfloat16)
 
 
 def attend_chunk(r, chip, q_lat, rope_q, recv, kr_out, acc, top, total, own_lens, attn_scale):
@@ -46,7 +56,7 @@
     return mixed, new_total
 
 
-def exchange_kernel(n, lens_hbm, lens_row_hbm, gain_hbm, cos_hbm, sin_hbm, c_hbm, k_hbm, ql_hbm, qr_hbm, recv, kr_out, acc, top, total, q_lat, rope_q, own_lens, lens, lens_row, gain_ref, cos_ref, sin_ref, send, k_raw, rot, turned, kr_send, kr_recv, q_rope, small_sem, load_sem, send_sem, recv_sem, kr_send_sem, kr_recv_sem):
+def exchange_kernel(n, lens_hbm, lens_row_hbm, gain_hbm, cos_hbm, sin_hbm, c_hbm, k_hbm, ql_hbm, qr_hbm, recv, kr_out, acc, top, total, q_lat, rope_q, own_lens, lens, lens_row, gain_ref, cos_ref, sin_ref, send, k_raw, rot, turned, kr_send, kr_recv, q_rope, small_sem, load_sem, send_sem, recv_sem, kr_send_sem, kr_recv_sem, ready):
     me = lax.axis_index("x")
     chips = n // 2
     my_chip, my_core = me // 2, lax.rem(me, 2)
@@ -64,9 +74,14 @@
             partners.append((dist, core))
     targets = [device(*partner) for partner in partners]
 
+    near = [device(dist, core) for dist, core in ((1, 0), (-1, 0), (1, 1), (-1, 1), (0, 1))]
+
+    def greet(sem):
+        for target in near:
+            pl.semaphore_signal(sem, inc=1, device_id={"x": target}, device_id_type=MESH)
+
     barrier = pltpu.get_barrier_semaphore()
-    for target in targets:
-        pl.semaphore_signal(barrier, inc=1, device_id={"x": target}, device_id_type=MESH)
+    greet(barrier)
 
     def load_c(i):
         dest = me if i == n - 1 else targets[i]
@@ -76,27 +91,19 @@
     small = [pltpu.make_async_copy(src, dst, small_sem.at[i]) for i, (src, dst) in enumerate(small)]
     for copy in small[:2]:
         copy.start()
-    for i in range(4):
+    for i in range(RAW, RAW + 3):
         load_c(i).start()
     for copy in small[2:]:
         copy.start()
-    for i in range(4, n):
+    for i in range(RAW + 3, n):
         load_c(i).start()
-    for copy in small[:2]:
-        copy.wait()
-
-    gain = gain_ref[...].astype(jnp.float32).reshape(1, rank)
-    row_pos = me * seq_local + lax.broadcasted_iota(jnp.int32, (seq_local, 1), 0)
 
     def norm_rows(i):
         load_c(i).wait()
         dest = me if i == n - 1 else targets[i]
 
         def one(slot, carry):
-            rows = send[dest, slot].astype(jnp.float32)
-            inv_rms = lax.rsqrt(jnp.mean(rows * rows, axis=-1, keepdims=True) + NORM_EPS)
-            valid = row_pos < lens[dest * slots + slot]
-            normed = jnp.where(valid, rows * inv_rms * gain, 0.0).astype(jnp.bfloat16)
+            normed = normed_rows(send[dest, slot], gain, me * seq_local, lens[dest * slots + slot])
             if i == n - 1:
                 recv[slot, pl.ds(pl.multiple_of(me * seq_local, seq_local), seq_local), :] = normed
             else:
@@ -109,7 +116,7 @@
         dist, core, first, count = messages[m]
         target = device(dist, core)
         return pltpu.make_async_remote_copy(
-            src_ref=send.at[target, pl.ds(first, count)],
+            src_ref=(c_hbm if m < RAW else send).at[target, pl.ds(first, count)],
             dst_ref=recv.at[pl.ds(first, count), pl.ds(pl.multiple_of(me * seq_local, seq_local), seq_local)],
             send_sem=send_sem.at[m],
             recv_sem=recv_sem.at[m],
@@ -132,15 +139,21 @@
             if (dist, core) == partners[i]:
                 c_copy(m).start()
 
+    pl.semaphore_wait(barrier, len(near))
+    for i in range(RAW):
+        send_rows(i)
+    greet(ready.at[0])
+    for copy in small[:2]:
+        copy.wait()
+    gain = gain_ref[...].astype(jnp.float32).reshape(1, rank)
     early = 5
-    norm_rows(0)
-    norm_rows(1)
-    pl.semaphore_wait(barrier, n - 1)
-    for i in range(2, early):
-        send_rows(i - 2)
+    for i in range(RAW, early):
         norm_rows(i)
-    send_rows(early - 2)
-    send_rows(early - 1)
+        send_rows(i)
+    for stage in range(chips // 2 - 1):
+        pl.semaphore_wait(ready.at[stage], len(near))
+        if stage + 1 < chips // 2 - 1:
+            greet(ready.at[stage + 1])
 
     for copy in small[2:]:
         copy.wait()
@@ -194,9 +207,17 @@
         for m, (far, _, _, _) in enumerate(messages):
             if (far + dist) % chips == 0:
                 c_copy(m).wait_recv()
+                if m < RAW:
+                    first_pos = pl.multiple_of((2 * chip + lax.rem(my_core + messages[m][1], 2)) * seq_local, seq_local)
+
+                    def one(slot, carry, first_pos=first_pos):
+                        recv[slot, pl.ds(first_pos, seq_local), :] = normed_rows(recv[slot, pl.ds(first_pos, seq_local), :], gain, first_pos, lens[me * slots + slot])
+                        return carry
+
+                    lax.fori_loop(0, slots, one, 0, unroll=2)
         return chip
 
-    for dist in [0] + [sign * far for far in range(1, chips // 2) for sign in (1, -1)]:
+    for dist in [0] + [sign * far for far in DISTANCES for sign in (1, -1)]:
         chip = gather_chip(dist)
 
         def one_request(r, carry, chip=chip):
@@ -291,6 +312,7 @@
                 pltpu.SemaphoreType.DMA((messages,)),
                 pltpu.SemaphoreType.DMA((n - 1,)),
                 pltpu.SemaphoreType.DMA((n - 1,)),
+                pltpu.SemaphoreType.REGULAR((n // 4 - 1,)),
             ],
             compiler_params=pltpu.CompilerParams(collective_id=0, has_side_effects=True, vmem_limit_bytes=40 * 1024 * 1024),
             name="exchange",

time: 222 us -> 224 us (level); the launches traced: 222 us -> 221 us
  no operation moved by 1% of the time
where the time goes in v3:
time: 224 us; the launch traced here: 221 us
  Pallas kernels  220 us (98%)
    pallas_call x1, Pallas kernels, local_step(): pl.pallas_call(functools.partial(exchange_kernel, n), out_shape=[pltpu.VM...  216 us

profile of v3, /device:TPU:21, one launch (start us, length us, event | category | flops | bytes accessed | tf_op | source)
XLA Modules:
  0.0 221.1 jit_solution(5665123464505452365)
XLA Ops:
  0.6 216.4 %exchange.1 = (bf16[8,1024,512]{2,1,0:T(8,128)(2,1)S(1)}, bf16[8,64,1024]{2,1,0:T(8,128)(2,1)S(1)}, f32[8,128,512]{2,1,0:T(8,128)S(1)}, f32[8,128,1]{2,1,0:T(8,1...) custom-call(s32[128]{0:T(128)} %lens_hbm.1, ...), custom_call_target="tpu_custom_call" | custom-call | tf_op jit(solution)/shard_map/exchange/pallas_call | solution.py:291
  217.1 4.0 %finish.1 = (bf16[8,1024,512]{2,1,0:T(8,128)(2,1)}, bf16[8,64,1024]{2,1,0:T(8,128)(2,1)}, bf16[8,128,512]{2,1,0:T(8,128)(2,1)}) custom-call(bf16[8,1024,512]{2,1,0:T(8,128)(2,1)S(1)} %get-tuple-element.14.recv, bf16[8,64,1024]{2,1,0:T(8,128)(2,1)S(1)} %get-tuple-element.15.kr_in, f32[8,128,512]{2,1,0:T(8,128)S(1)} %get-tuple-element.16.acc, ...), custom_call_target="tpu_custom_call" | custom-call | tf_op jit(solution)/shard_map/finish/pallas_call | solution.py:321

commit v4 on v3

--- a/solution.py
+++ b/solution.py
@@ -10,21 +10,19 @@
 NORM_EPS = 1e-6
 MASKED = -3.0e38
 MESH = pl.DeviceIdType.MESH
-DISTANCES = (1, 3, 2)
+DISTANCES = (3, 2, 1)
 RAW = 2
 
 
 def message_order(chips, slots):
-    far = chips // 2
     order = []
     for dist in DISTANCES:
         for core in (0, 1):
             for sign in (1, -1):
                 order.append((sign * dist, core, 0, slots))
     order.insert(4, (0, 1, 0, slots))
-    for first in (0, slots // 2):
-        for core in (0, 1):
-            order.append((far, core, first, slots // 2))
+    for core in (0, 1):
+        order.append((chips // 2, core, 0, slots))
     return order
 
 
@@ -56,7 +54,7 @@
     return mixed, new_total
 
 
-def exchange_kernel(n, lens_hbm, lens_row_hbm, gain_hbm, cos_hbm, sin_hbm, c_hbm, k_hbm, ql_hbm, qr_hbm, recv, kr_out, acc, top, total, q_lat, rope_q, own_lens, lens, lens_row, gain_ref, cos_ref, sin_ref, send, k_raw, rot, turned, kr_send, kr_recv, q_rope, small_sem, load_sem, send_sem, recv_sem, kr_send_sem, kr_recv_sem, ready):
+def exchange_kernel(n, lens_hbm, lens_row_hbm, gain_hbm, cos_hbm, sin_hbm, c_hbm, k_hbm, ql_hbm, qr_hbm, recv, kr_out, acc, top, total, q_lat, rope_q, own_lens, lens, lens_row, gain_ref, cos_ref, sin_ref, send, k_raw, rot, turned, kr_send, kr_recv, q_rope, small_sem, load_sem, send_sem, recv_sem, kr_send_sem, kr_recv_sem):
     me = lax.axis_index("x")
     chips = n // 2
     my_chip, my_core = me // 2, lax.rem(me, 2)
@@ -74,14 +72,9 @@
             partners.append((dist, core))
     targets = [device(*partner) for partner in partners]
 
-    near = [device(dist, core) for dist, core in ((1, 0), (-1, 0), (1, 1), (-1, 1), (0, 1))]
-
-    def greet(sem):
-        for target in near:
-            pl.semaphore_signal(sem, inc=1, device_id={"x": target}, device_id_type=MESH)
-
     barrier = pltpu.get_barrier_semaphore()
-    greet(barrier)
+    for target in targets:
+        pl.semaphore_signal(barrier, inc=1, device_id={"x": target}, device_id_type=MESH)
 
     def load_c(i):
         dest = me if i == n - 1 else targets[i]
@@ -89,28 +82,17 @@
 
     small = [(lens_hbm, lens), (gain_hbm, gain_ref), (lens_row_hbm, lens_row), (cos_hbm, cos_ref), (sin_hbm, sin_ref), (k_hbm, k_raw), (qr_hbm, q_rope), (ql_hbm, q_lat)]
     small = [pltpu.make_async_copy(src, dst, small_sem.at[i]) for i, (src, dst) in enumerate(small)]
-    for copy in small[:2]:
-        copy.start()
-    for i in range(RAW, RAW + 3):
-        load_c(i).start()
-    for copy in small[2:]:
-        copy.start()
-    for i in range(RAW + 3, n):
-        load_c(i).start()
-
-    def norm_rows(i):
-        load_c(i).wait()
-        dest = me if i == n - 1 else targets[i]
-
+
+    def norm_rows(dest, first, count):
         def one(slot, carry):
             normed = normed_rows(send[dest, slot], gain, me * seq_local, lens[dest * slots + slot])
-            if i == n - 1:
+            if dest is me:
                 recv[slot, pl.ds(pl.multiple_of(me * seq_local, seq_local), seq_local), :] = normed
             else:
                 send[dest, slot] = normed
             return carry
 
-        lax.fori_loop(0, slots, one, 0, unroll=2)
+        lax.fori_loop(first, first + count, one, 0, unroll=2)
 
     def c_copy(m):
         dist, core, first, count = messages[m]
@@ -134,28 +116,34 @@
             device_id_type=MESH,
         )
 
-    def send_rows(i):
-        for m, (dist, core, _, _) in enumerate(messages):
-            if (dist, core) == partners[i]:
-                c_copy(m).start()
-
-    pl.semaphore_wait(barrier, len(near))
-    for i in range(RAW):
-        send_rows(i)
-    greet(ready.at[0])
+    loaded = []
+
+    def send_rows(m):
+        dist, core, first, count = messages[m]
+        if m >= RAW:
+            i = partners.index((dist, core))
+            if i not in loaded:
+                load_c(i).wait()
+                loaded.append(i)
+            norm_rows(targets[i], first, count)
+        c_copy(m).start()
+        if m >= RAW and first == 0:
+            kr_copy(partners.index((dist, core))).start()
+
     for copy in small[:2]:
-        copy.wait()
-    gain = gain_ref[...].astype(jnp.float32).reshape(1, rank)
-    early = 5
-    for i in range(RAW, early):
-        norm_rows(i)
-        send_rows(i)
-    for stage in range(chips // 2 - 1):
-        pl.semaphore_wait(ready.at[stage], len(near))
-        if stage + 1 < chips // 2 - 1:
-            greet(ready.at[stage + 1])
-
+        copy.start()
+    loads = [i for i in range(n) if i == n - 1 or any(partners[i] == message[:2] for message in messages[RAW:])]
+    for i in loads[:3]:
+        load_c(i).start()
     for copy in small[2:]:
+        copy.start()
+    for i in loads[3:]:
+        load_c(i).start()
+
+    pl.semaphore_wait(barrier, n - 1)
+    for m in range(RAW):
+        send_rows(m)
+    for copy in small:
         copy.wait()
     lens_vec = lens_row[...]
     for pos in range(seq_local):
@@ -175,14 +163,13 @@
         kr_send[dest] = turned[dest * slots * half : (dest + 1) * slots * half, :].astype(jnp.bfloat16)
     kr_recv[me] = kr_send[me]
 
-    norm_rows(early)
-    for i in range(n - 1):
+    for i in range(RAW):
         kr_copy(i).start()
-    for i in range(early + 1, n - 1):
-        send_rows(i - 1)
-        norm_rows(i)
-    send_rows(n - 2)
-    norm_rows(n - 1)
+    gain = gain_ref[...].astype(jnp.float32).reshape(1, rank)
+    for m in range(RAW, len(messages)):
+        send_rows(m)
+    load_c(n - 1).wait()
+    norm_rows(me, 0, slots)
 
     for slot in range(slots):
         rope_q[slot] = q_rope[slot].astype(jnp.float32).T.astype(jnp.bfloat16)
@@ -214,7 +201,7 @@
                         recv[slot, pl.ds(first_pos, seq_local), :] = normed_rows(recv[slot, pl.ds(first_pos, seq_local), :], gain, first_pos, lens[me * slots + slot])
                         return carry
 
-                    lax.fori_loop(0, slots, one, 0, unroll=2)
+                    lax.fori_loop(messages[m][2], sum(messages[m][2:]), one, 0, unroll=2)
         return chip
 
     for dist in [0] + [sign * far for far in DISTANCES for sign in (1, -1)]:
@@ -312,7 +299,6 @@
                 pltpu.SemaphoreType.DMA((messages,)),
                 pltpu.SemaphoreType.DMA((n - 1,)),
                 pltpu.SemaphoreType.DMA((n - 1,)),
-                pltpu.SemaphoreType.REGULAR((n // 4 - 1,)),
             ],
             compiler_params=pltpu.CompilerParams(collective_id=0, has_side_effects=True, vmem_limit_bytes=40 * 1024 * 1024),
             name="exchange",

time: 224 us -> 218 us (0.973); the launches traced: 221 us -> 218 us
  Pallas kernels: 220 us -> 217 us
    pallas_call x1, Pallas kernels: 216 us -> 213 us  [local_step(): pl.pallas_call(functools.partial(exchange_kernel, n), out_shape=[pltpu.VM...]
where the time goes in v4:
time: 218 us
  Pallas kernels  217 us (100%)
    pallas_call x1, Pallas kernels, local_step(): pl.pallas_call(functools.partial(exchange_kernel, n), out_shape=[pltpu.VM...  213 us

profile of v4, /device:TPU:21, one launch (start us, length us, event | category | flops | bytes accessed | tf_op | source)
XLA Modules:
  0.0 217.8 jit_solution(17492541420486811904)
XLA Ops:
  0.6 213.1 %exchange.1 = (bf16[8,1024,512]{2,1,0:T(8,128)(2,1)S(1)}, bf16[8,64,1024]{2,1,0:T(8,128)(2,1)S(1)}, f32[8,128,512]{2,1,0:T(8,128)S(1)}, f32[8,128,1]{2,1,0:T(8,1...) custom-call(s32[128]{0:T(128)} %lens_hbm.1, ...), custom_call_target="tpu_custom_call" | custom-call | tf_op jit(solution)/shard_map/exchange/pallas_call | solution.py:278
  213.7 4.0 %finish.1 = (bf16[8,1024,512]{2,1,0:T(8,128)(2,1)}, bf16[8,64,1024]{2,1,0:T(8,128)(2,1)}, bf16[8,128,512]{2,1,0:T(8,128)(2,1)}) custom-call(bf16[8,1024,512]{2,1,0:T(8,128)(2,1)S(1)} %get-tuple-element.14.recv, bf16[8,64,1024]{2,1,0:T(8,128)(2,1)S(1)} %get-tuple-element.15.kr_in, f32[8,128,512]{2,1,0:T(8,128)S(1)} %get-tuple-element.16.acc, ...), custom_call_target="tpu_custom_call" | custom-call | tf_op jit(solution)/shard_map/finish/pallas_call | solution.py:307

commit v5 on v4

--- a/solution.py
+++ b/solution.py
@@ -78,7 +78,7 @@
 
     def load_c(i):
         dest = me if i == n - 1 else targets[i]
-        return pltpu.make_async_copy(c_hbm.at[dest], send.at[dest], load_sem.at[i])
+        return pltpu.make_async_copy(c_hbm.at[dest], send.at[dest], load_sem.at[0])
 
     small = [(lens_hbm, lens), (gain_hbm, gain_ref), (lens_row_hbm, lens_row), (cos_hbm, cos_ref), (sin_hbm, sin_ref), (k_hbm, k_raw), (qr_hbm, q_rope), (ql_hbm, q_lat)]
     small = [pltpu.make_async_copy(src, dst, small_sem.at[i]) for i, (src, dst) in enumerate(small)]
@@ -100,8 +100,8 @@
         return pltpu.make_async_remote_copy(
             src_ref=(c_hbm if m < RAW else send).at[target, pl.ds(first, count)],
             dst_ref=recv.at[pl.ds(first, count), pl.ds(pl.multiple_of(me * seq_local, seq_local), seq_local)],
-            send_sem=send_sem.at[m],
-            recv_sem=recv_sem.at[m],
+            send_sem=send_sem.at[0],
+            recv_sem=recv_sem.at[dist % chips],
             device_id={"x": target},
             device_id_type=MESH,
         )
@@ -110,25 +110,22 @@
         return pltpu.make_async_remote_copy(
             src_ref=kr_send.at[targets[i]],
             dst_ref=kr_recv.at[me],
-            send_sem=kr_send_sem.at[i],
-            recv_sem=kr_recv_sem.at[i],
+            send_sem=kr_send_sem.at[0],
+            recv_sem=kr_recv_sem.at[partners[i][0] % chips],
             device_id={"x": targets[i]},
             device_id_type=MESH,
         )
 
-    loaded = []
+    def wait_for(region, sem):
+        pltpu.make_async_copy(region, region, sem).wait()
 
     def send_rows(m):
         dist, core, first, count = messages[m]
         if m >= RAW:
             i = partners.index((dist, core))
-            if i not in loaded:
-                load_c(i).wait()
-                loaded.append(i)
             norm_rows(targets[i], first, count)
+            kr_copy(i).start()
         c_copy(m).start()
-        if m >= RAW and first == 0:
-            kr_copy(partners.index((dist, core))).start()
 
     for copy in small[:2]:
         copy.start()
@@ -166,9 +163,9 @@
     for i in range(RAW):
         kr_copy(i).start()
     gain = gain_ref[...].astype(jnp.float32).reshape(1, rank)
+    wait_for(send.at[pl.ds(0, len(loads))], load_sem.at[0])
     for m in range(RAW, len(messages)):
         send_rows(m)
-    load_c(n - 1).wait()
     norm_rows(me, 0, slots)
 
     for slot in range(slots):
@@ -182,18 +179,17 @@
 
     def gather_chip(dist):
         chip = lax.rem(my_chip + dist + chips, chips)
-        for i, (far, _) in enumerate(partners):
-            if (far + dist) % chips == 0:
-                kr_copy(i).wait_recv()
+        partner = device(0, 1)
+        wait_for(kr_recv.at[pl.ds(2 * chip, 2)] if dist else kr_recv.at[partner], kr_recv_sem.at[-dist % chips])
         start = pl.multiple_of(chip * 2 * seq_local, 2 * seq_local)
         for slot in range(slots):
             even = kr_recv[2 * chip, slot * half : (slot + 1) * half, :].astype(jnp.float32)
             odd = kr_recv[2 * chip + 1, slot * half : (slot + 1) * half, :].astype(jnp.float32)
             kr_out[slot, :half, pl.ds(start, 2 * seq_local)] = jnp.where(low_lanes, even, pltpu.roll(odd, seq_local, 1)).astype(jnp.bfloat16)
             kr_out[slot, half:, pl.ds(start, 2 * seq_local)] = jnp.where(low_lanes, pltpu.roll(even, seq_local, 1), odd).astype(jnp.bfloat16)
+        wait_for(recv.at[:, pl.ds(start, 2 * seq_local)] if dist else recv.at[:, pl.ds(pl.multiple_of(partner * seq_local, seq_local), seq_local)], recv_sem.at[-dist % chips])
         for m, (far, _, _, _) in enumerate(messages):
             if (far + dist) % chips == 0:
-                c_copy(m).wait_recv()
                 if m < RAW:
                     first_pos = pl.multiple_of((2 * chip + lax.rem(my_core + messages[m][1], 2)) * seq_local, seq_local)
 
@@ -213,11 +209,9 @@
 
         lax.fori_loop(0, slots, one_request, 0, unroll=2)
 
-    for i in range(n - 1):
-        kr_copy(i).wait_send()
     gather_chip(chips // 2)
-    for m in range(len(messages)):
-        c_copy(m).wait_send()
+    wait_for(kr_send.at[pl.ds(0, n - 1)], kr_send_sem.at[0])
+    wait_for(send.at[pl.ds(0, n - 1)], send_sem.at[0])
 
 
 def finish_kernel(n, attn_scale, recv, kr_in, acc, top_in, total_in, q_lat, rope_q, own_lens, c_out, kr_out, o_out, top, total, o_ref, sem):
@@ -253,7 +247,6 @@
         bf16, f32, i32 = jnp.bfloat16, jnp.float32, jnp.int32
         hbm = pl.BlockSpec(memory_space=pltpu.HBM)
         vmem = pl.BlockSpec(memory_space=pltpu.VMEM)
-        messages = len(message_order(n // 2, slots))
         passed = [
             ((slots, seq_len, rank), bf16),
             ((slots, rope_dim, seq_len), bf16),
@@ -294,11 +287,11 @@
                 pltpu.VMEM((n, slots * half, 2 * seq_local), bf16),
                 pltpu.VMEM((slots, rope_dim, heads), bf16),
                 pltpu.SemaphoreType.DMA((8,)),
-                pltpu.SemaphoreType.DMA((n,)),
-                pltpu.SemaphoreType.DMA((messages,)),
-                pltpu.SemaphoreType.DMA((messages,)),
-                pltpu.SemaphoreType.DMA((n - 1,)),
-                pltpu.SemaphoreType.DMA((n - 1,)),
+                pltpu.SemaphoreType.DMA((1,)),
+                pltpu.SemaphoreType.DMA((1,)),
+                pltpu.SemaphoreType.DMA((n // 2,)),
+                pltpu.SemaphoreType.DMA((1,)),
+                pltpu.SemaphoreType.DMA((n // 2,)),
             ],
             compiler_params=pltpu.CompilerParams(collective_id=0, has_side_effects=True, vmem_limit_bytes=40 * 1024 * 1024),
             name="exchange",

time: 218 us -> 217 us (level)
  no operation moved by 1% of the time
where the time goes in v5:
time: 217 us
  Pallas kernels  216 us (100%)
    pallas_call x1, Pallas kernels, local_step(): pl.pallas_call(functools.partial(exchange_kernel, n), out_shape=[pltpu.VM...  212 us

profile of v5, /device:TPU:21, one launch (start us, length us, event | category | flops | bytes accessed | tf_op | source)
XLA Modules:
  0.0 217.1 jit_solution(4046185700836978908)
XLA Ops:
  0.6 212.4 %exchange.1 = (bf16[8,1024,512]{2,1,0:T(8,128)(2,1)S(1)}, bf16[8,64,1024]{2,1,0:T(8,128)(2,1)S(1)}, f32[8,128,512]{2,1,0:T(8,128)S(1)}, f32[8,128,1]{2,1,0:T(8,1...) custom-call(s32[128]{0:T(128)} %lens_hbm.1, ...), custom_call_target="tpu_custom_call" | custom-call | tf_op jit(solution)/shard_map/exchange/pallas_call | solution.py:271
  213.1 4.0 %finish.1 = (bf16[8,1024,512]{2,1,0:T(8,128)(2,1)}, bf16[8,64,1024]{2,1,0:T(8,128)(2,1)}, bf16[8,128,512]{2,1,0:T(8,128)(2,1)}) custom-call(bf16[8,1024,512]{2,1,0:T(8,128)(2,1)S(1)} %get-tuple-element.14.recv, bf16[8,64,1024]{2,1,0:T(8,128)(2,1)S(1)} %get-tuple-element.15.kr_in, f32[8,128,512]{2,1,0:T(8,128)S(1)} %get-tuple-element.16.acc, ...), custom_call_target="tpu_custom_call" | custom-call | tf_op jit(solution)/shard_map/finish/pallas_call | solution.py:300

commit v6 on v5

--- a/solution.py
+++ b/solution.py
@@ -217,20 +217,18 @@
 def finish_kernel(n, attn_scale, recv, kr_in, acc, top_in, total_in, q_lat, rope_q, own_lens, c_out, kr_out, o_out, top, total, o_ref, sem):
     chips = n // 2
     slots = acc.shape[0]
-    copies = [pltpu.make_async_copy(recv.at[r], c_out.at[r], sem.at[r]) for r in range(slots)]
-    copies.append(pltpu.make_async_copy(kr_in, kr_out, sem.at[slots]))
-    for copy in copies:
-        copy.start()
+    for r in range(slots):
+        pltpu.make_async_copy(recv.at[r], c_out.at[r], sem.at[0]).start()
+    pltpu.make_async_copy(kr_in, kr_out, sem.at[1]).start()
     top[...] = top_in[...]
     total[...] = total_in[...]
     chip = lax.rem(lax.axis_index("x") // 2 + chips // 2, chips)
     for r in range(slots):
         mixed, weight_sum = attend_chunk(r, chip, q_lat, rope_q, recv, kr_in, acc, top, total, own_lens, attn_scale)
         o_ref[r] = (mixed / weight_sum).astype(jnp.bfloat16)
-        copies.append(pltpu.make_async_copy(o_ref.at[r], o_out.at[r], sem.at[slots + 1 + r]))
-        copies[-1].start()
-    for copy in copies:
-        copy.wait()
+        pltpu.make_async_copy(o_ref.at[r], o_out.at[r], sem.at[2]).start()
+    for i, (src, dst) in enumerate([(recv, c_out), (kr_in, kr_out), (o_ref, o_out)]):
+        pltpu.make_async_copy(src, dst, sem.at[i]).wait()
 
 
 def solution(mesh):
@@ -306,7 +304,7 @@
                 pltpu.VMEM((slots, heads, 1), f32),
                 pltpu.VMEM((slots, heads, 1), f32),
                 pltpu.VMEM((slots, heads, rank), bf16),
-                pltpu.SemaphoreType.DMA((2 * slots + 1,)),
+                pltpu.SemaphoreType.DMA((3,)),
             ],
             compiler_params=pltpu.CompilerParams(vmem_limit_bytes=8 * 1024 * 1024),
             name="finish",

time: 217 us -> 217 us (level)
  no operation moved by 1% of the time
where the time goes in v6:
time: 217 us
  Pallas kernels  216 us (100%)
    pallas_call x1, Pallas kernels, local_step(): pl.pallas_call(functools.partial(exchange_kernel, n), out_shape=[pltpu.VM...  212 us

profile of v6, /device:TPU:21, one launch (start us, length us, event | category | flops | bytes accessed | tf_op | source)
XLA Modules:
  0.0 217.0 jit_solution(11420498810095130335)
XLA Ops:
  0.6 212.4 %exchange.1 = (bf16[8,1024,512]{2,1,0:T(8,128)(2,1)S(1)}, bf16[8,64,1024]{2,1,0:T(8,128)(2,1)S(1)}, f32[8,128,512]{2,1,0:T(8,128)S(1)}, f32[8,128,1]{2,1,0:T(8,1...) custom-call(s32[128]{0:T(128)} %lens_hbm.1, ...), custom_call_target="tpu_custom_call" | custom-call | tf_op jit(solution)/shard_map/exchange/pallas_call | solution.py:269
  213.1 3.9 %finish.1 = (bf16[8,1024,512]{2,1,0:T(8,128)(2,1)}, bf16[8,64,1024]{2,1,0:T(8,128)(2,1)}, bf16[8,128,512]{2,1,0:T(8,128)(2,1)}) custom-call(bf16[8,1024,512]{2,1,0:T(8,128)(2,1)S(1)} %get-tuple-element.14.recv, bf16[8,64,1024]{2,1,0:T(8,128)(2,1)S(1)} %get-tuple-element.15.kr_in, f32[8,128,512]{2,1,0:T(8,128)S(1)} %get-tuple-element.16.acc, ...), custom_call_target="tpu_custom_call" | custom-call | tf_op jit(solution)/shard_map/finish/pallas_call | solution.py:298

commit v7 on v6

--- a/solution.py
+++ b/solution.py
@@ -18,7 +18,7 @@
     order = []
     for dist in DISTANCES:
         for core in (0, 1):
-            for sign in (1, -1):
+            for sign in (-1, 1):
                 order.append((sign * dist, core, 0, slots))
     order.insert(4, (0, 1, 0, slots))
     for core in (0, 1):

time: 217 us -> 217 us (level)
  no operation moved by 1% of the time
where the time goes in v7:
time: 217 us
  Pallas kernels  216 us (100%)
    pallas_call x1, Pallas kernels, local_step(): pl.pallas_call(functools.partial(exchange_kernel, n), out_shape=[pltpu.VM...  212 us

profile of v7, /device:TPU:21, one launch (start us, length us, event | category | flops | bytes accessed | tf_op | source)
XLA Modules:
  0.0 216.9 jit_solution(5087932174701770464)
XLA Ops:
  0.6 212.4 %exchange.1 = (bf16[8,1024,512]{2,1,0:T(8,128)(2,1)S(1)}, bf16[8,64,1024]{2,1,0:T(8,128)(2,1)S(1)}, f32[8,128,512]{2,1,0:T(8,128)S(1)}, f32[8,128,1]{2,1,0:T(8,1...) custom-call(s32[128]{0:T(128)} %lens_hbm.1, ...), custom_call_target="tpu_custom_call" | custom-call | tf_op jit(solution)/shard_map/exchange/pallas_call | solution.py:269
  213.0 3.9 %finish.1 = (bf16[8,1024,512]{2,1,0:T(8,128)(2,1)}, bf16[8,64,1024]{2,1,0:T(8,128)(2,1)}, bf16[8,128,512]{2,1,0:T(8,128)(2,1)}) custom-call(bf16[8,1024,512]{2,1,0:T(8,128)(2,1)S(1)} %get-tuple-element.14.recv, bf16[8,64,1024]{2,1,0:T(8,128)(2,1)S(1)} %get-tuple-element.15.kr_in, f32[8,128,512]{2,1,0:T(8,128)S(1)} %get-tuple-element.16.acc, ...), custom_call_target="tpu_custom_call" | custom-call | tf_op jit(solution)/shard_map/finish/pallas_call | solution.py:298
